TPU v7x, 256 devices: a 8x8x2 block of a 8x8x16 slice. The times are simulated.
256 devices in a mesh: parts: 2 (over z), seq: 128 (over x, y, core).
Axes of the slice: x: 8, y: 8, z: 2, core: 2. Of those that a mesh axis runs over, the one named last changes fastest.
The devices are a block of a 8x8x16 slice.
Arguments:
- token_ids: int32 [4, 4], P(None, 'parts'), parts along dimension 1, may hold values from 0 to 76031
- lengths: int32 [4], P('parts'), parts along dimension 0, may hold values from 24576 to 32768, as said below
- embed_table: bfloat16 [76032, 5120], P('seq'), may hold values from -6 to 6
- attn_gain: bfloat16 [5120], replicated, may hold values from 0.25 to 1.75
- w_qkv: bfloat16 [5120, 7168], P('seq'), may hold values from -0.3125 to 0.3125
- qkv_bias: float32 [7168], replicated, may hold values from -8 to 8
- cache_keys: bfloat16 [4, 32768, 1024], P('parts', 'seq'), parts along dimension 0, may hold values from -300 to 300
- cache_values: bfloat16 [4, 32768, 1024], P('parts', 'seq'), parts along dimension 0, may hold values from -6 to 6
- w_out: bfloat16 [5120, 5120], P(None, 'seq'), may hold values from -0.078125 to 0.078125
- mlp_gain: bfloat16 [5120], replicated, may hold values from 0.25 to 1.75
- w_gate: bfloat16 [5120, 16384], P(None, 'seq'), may hold values from -0.078125 to 0.078125
- w_up: bfloat16 [5120, 16384], P(None, 'seq'), may hold values from -0.078125 to 0.078125
- w_down: bfloat16 [16384, 5120], P('seq'), may hold values from -0.1875 to 0.1875
Outputs:
- attended: bfloat16 [4, 4, 5120], P(None, 'parts'), parts along dimension 1
- layer_out: bfloat16 [4, 4, 5120], P(None, 'parts', 'seq'), parts along dimension 1
There are 2 independent parts, one for each index of `parts`. A program takes and returns all parts, laid end to end along the dimension named above; an argument that names none is the same for every part. Nothing has to cross between parts.
Inputs may be any that keep to these rules, and one draw needn't show every extreme that they name: Cache positions lengths[b] and later are unused; the first prompt fills the whole cache of 32768 positions.
All inputs are finite; a program needn't handle non-finite values.
Results may differ from a plain program's by a relative error of at most 0.017.
The roundings to bfloat16 on the way count: a program that leaves them out, or rounds other values in their place, can miss the bound.
Values may be sent and summed in bfloat16 or wider, within the bound.
No kernel may reach another device: no remote copies, remote signals or barrier semaphores. Data moves between devices by JAX's collectives and lax.ppermute only.
A program may use at most 128 MiB of HBM per device.

v0:
```python
import math
import jax
import jax.numpy as jnp
from jax import lax
from jax.sharding import Mesh
from jax.sharding import PartitionSpec as P

HEADS = 40
KV_HEADS = 8
HEAD_DIM = 128
SEQ = ("seq_0", "seq_1", "seq_2")
NORM_EPS = 1e-06
ROPE_BASE = 1000000.0
MASKED = -1e30


def gathered_once(array, axis):
    leaves = jax.tree.leaves(array)
    order = sorted(range(len(leaves)), key=lambda k: -leaves[k].size)
    width = (1, *leaves[order[0]].shape)[-1]
    lines = [
        jnp.pad(leaves[k].reshape(-1), (0, -leaves[k].size % width)).reshape(-1, width)
        for k in order
    ]
    both, at, found = (lax.all_gather(jnp.concatenate(lines), axis), 0, {})
    for k, line in zip(order, lines):
        slab = both[:, at : at + len(line)].reshape(len(both), -1)
        found[k] = slab[:, : leaves[k].size].reshape(-1, *leaves[k].shape)
        at += len(line)
    numbers = iter(range(len(leaves)))
    return jax.tree.map(lambda _: found[next(numbers)], array)


def combined_by_axis(array, axes, combine):
    for axis in axes:
        pieces = gathered_once(array, axis)
        array = jax.tree.map(lambda part: part[0], pieces)
        for k in range(1, lax.axis_size(axis)):
            array = combine(array, jax.tree.map(lambda part: part[k], pieces))
    return array


def sum_in_order(parts, axes, order):
    dims = [lax.axis_size(a) for a in axes]
    parts = parts.reshape(*dims, *parts.shape[1:])
    parts = parts.transpose(*order, *range(len(axes), parts.ndim))
    parts = parts.reshape(-1, *parts.shape[len(axes) :])
    for k in order:
        parts = lax.psum_scatter(parts, axes[k], scatter_dimension=0, tiled=True)
    return parts[0]


def cut_along(array, dim, devices):
    before, after = (array.shape[:dim], array.shape[dim + 1 :])
    return jnp.moveaxis(array.reshape(*before, devices, -1, *after), dim, 0)


def scatter_axes(array, axes, order, dim):
    devices = lax.axis_size(axes)
    return sum_in_order(cut_along(array, dim, devices), axes, order)


def rms_normalize(rows, gain):
    mean_square = jnp.mean(rows * rows, axis=-1, keepdims=True)
    return (rows * lax.rsqrt(mean_square + NORM_EPS) * gain.astype(jnp.float32)).astype(
        jnp.bfloat16
    )


def rotate(vectors, positions):
    half_dim = vectors.shape[-1] // 2
    frequency = ROPE_BASE ** (-2.0 * jnp.arange(half_dim, dtype=jnp.float32) / vectors.shape[-1])
    angles = positions.astype(jnp.float32)[..., None, None] * frequency
    cosine = jnp.cos(angles)
    sine_part = jnp.sin(angles)
    widened = vectors.astype(jnp.float32)
    first_half = widened[..., :half_dim]
    second = widened[..., half_dim:]
    joined = jnp.concatenate(
        [first_half * cosine - second * sine_part, second * cosine + first_half * sine_part],
        axis=-1,
    )
    return joined.astype(jnp.bfloat16)


def combine_partials(earlier, latter):
    top_one, total_one, sum_one = earlier
    top_two, total_two, sum_two = latter
    joined_top = jnp.maximum(top_one, top_two)
    scale_one = jnp.exp(top_one - joined_top)
    scale_two = jnp.exp(top_two - joined_top)
    return (
        joined_top,
        total_one * scale_one + total_two * scale_two,
        sum_one * scale_one[..., None] + sum_two * scale_two[..., None],
    )


def body(
    token_ids,
    lengths,
    embed_table,
    attn_gain,
    w_qkv,
    qkv_bias,
    cache_keys,
    cache_values,
    w_out,
    mlp_gain,
    w_gate,
    w_up,
    w_down,
):
    rank = lax.axis_index(SEQ)
    step_count, batch_count = token_ids.shape
    model_width = embed_table.shape[1]
    vocab_rows = embed_table.shape[0]
    query_width = HEADS * HEAD_DIM
    key_width = KV_HEADS * HEAD_DIM
    group_size = HEADS // KV_HEADS
    local_ids = token_ids - rank * vocab_rows
    inside = (local_ids >= 0) & (local_ids < vocab_rows)
    picked = jnp.take(embed_table, jnp.clip(local_ids, 0, vocab_rows - 1), axis=0)
    partial_rows = jnp.where(inside[..., None], picked.astype(jnp.float32), 0.0)
    stream = lax.psum(partial_rows, SEQ)
    normed = rms_normalize(stream, attn_gain).reshape(-1, model_width)
    feature_rows = w_qkv.shape[0]
    normed_local = lax.dynamic_slice_in_dim(normed, rank * feature_rows, feature_rows, 1)
    joint_partial = jnp.dot(normed_local, w_qkv, preferred_element_type=jnp.float32)
    joint_summed = lax.psum(joint_partial, SEQ)
    joint = (joint_summed + qkv_bias).astype(jnp.bfloat16).reshape(step_count, batch_count, -1)
    query_part = joint[..., :query_width].reshape(step_count, batch_count, HEADS, HEAD_DIM)
    key_part = joint[..., query_width : query_width + key_width].reshape(
        step_count, batch_count, KV_HEADS, HEAD_DIM
    )
    value_part = joint[..., query_width + key_width :].reshape(
        step_count, batch_count, KV_HEADS, HEAD_DIM
    )
    positions = lengths[None, :] + jnp.arange(step_count, dtype=jnp.int32)[:, None]
    queries = rotate(query_part, positions)
    new_keys = rotate(key_part, positions)
    grouped = queries.reshape(step_count, batch_count, KV_HEADS, group_size, HEAD_DIM)
    score_scale = 1.0 / math.sqrt(HEAD_DIM)
    local_len = cache_keys.shape[1]
    key_blocks = cache_keys.reshape(batch_count, local_len, KV_HEADS, HEAD_DIM)
    value_blocks = cache_values.reshape(batch_count, local_len, KV_HEADS, HEAD_DIM)
    scores = (
        jnp.einsum("sbkgd,bpkd->bkgsp", grouped, key_blocks, preferred_element_type=jnp.float32)
        * score_scale
    )
    places = rank * local_len + jnp.arange(local_len, dtype=jnp.int32)
    valid = (places[None, :] < lengths[:, None])[:, None, None, None, :]
    masked = jnp.where(valid, scores, MASKED)
    local_top = jnp.max(masked, axis=-1)
    weights = jnp.where(valid, jnp.exp(masked - local_top[..., None]), 0.0)
    local_total = jnp.sum(weights, axis=-1)
    local_sum = jnp.einsum(
        "bkgsp,bpkd->bkgsd",
        weights.astype(jnp.bfloat16),
        value_blocks,
        preferred_element_type=jnp.float32,
    )
    merged_top, merged_total, merged_sum = combined_by_axis(
        (local_top, local_total, local_sum), SEQ, combine_partials
    )
    new_scores = (
        jnp.einsum("sbkgd,tbkd->bkgst", grouped, new_keys, preferred_element_type=jnp.float32)
        * score_scale
    )
    step_index = jnp.arange(step_count, dtype=jnp.int32)
    causal = step_index[:, None] >= step_index[None, :]
    new_masked = jnp.where(causal, new_scores, MASKED)
    final_top = jnp.maximum(merged_top, jnp.max(new_masked, axis=-1))
    rescale = jnp.exp(merged_top - final_top)
    new_weights = jnp.where(causal, jnp.exp(new_masked - final_top[..., None]), 0.0)
    final_total = merged_total * rescale + jnp.sum(new_weights, axis=-1)
    final_sum = merged_sum * rescale[..., None] + jnp.einsum(
        "bkgst,tbkd->bkgsd",
        new_weights.astype(jnp.bfloat16),
        value_part,
        preferred_element_type=jnp.float32,
    )
    attended = jnp.transpose(final_sum / final_total[..., None], (3, 0, 1, 2, 4))
    attended = attended.reshape(step_count, batch_count, query_width).astype(jnp.bfloat16)
    shard_cols = w_out.shape[1]
    projected = jnp.dot(
        attended.reshape(-1, query_width), w_out, preferred_element_type=jnp.float32
    )
    stream_shard = lax.dynamic_slice_in_dim(stream, rank * shard_cols, shard_cols, 2)
    mid_shard = stream_shard + projected.reshape(step_count, batch_count, shard_cols)
    mid_rows = lax.all_gather(mid_shard, SEQ, axis=2, tiled=True)
    normed_mid = rms_normalize(mid_rows, mlp_gain)
    flat_rows = normed_mid.reshape(-1, model_width)
    gate = jnp.dot(flat_rows, w_gate, preferred_element_type=jnp.float32)
    upper = jnp.dot(flat_rows, w_up, preferred_element_type=jnp.float32)
    hidden = (jax.nn.silu(gate) * upper).astype(jnp.bfloat16)
    down_terms = jnp.dot(hidden, w_down, preferred_element_type=jnp.float32).reshape(
        step_count, batch_count, model_width
    )
    summed = scatter_axes(down_terms, SEQ, (2, 1, 0), 2)
    layer_out = (mid_shard + summed).astype(jnp.bfloat16)
    return (attended, layer_out)


def solution(mesh):
    finer = Mesh(
        mesh.devices.reshape(mesh.shape["parts"], 8, 8, 2), ("parts", "seq_0", "seq_1", "seq_2")
    )
    return jax.shard_map(
        body,
        mesh=finer,
        in_specs=(
            P(None, "parts"),
            P("parts"),
            P(SEQ, None),
            P(),
            P(SEQ, None),
            P(),
            P("parts", SEQ, None),
            P("parts", SEQ, None),
            P(None, SEQ),
            P(),
            P(None, SEQ),
            P(None, SEQ),
            P(SEQ, None),
        ),
        out_specs=(P(None, "parts", None), P(None, "parts", SEQ)),
        check_vma=False,
    )
```

profile of v0, /device:TPU:528, one launch (start us, length us, event | category | flops | bytes accessed | tf_op | source)
XLA Modules:
  0.0 717.2 jit_solution(17745230185070453889)
XLA Ops:
  7.3 0.8 compare_and_fusion
  8.3 4.2 gather_fusion
  12.8 0.8 convert_select_fusion
  14.4 1.1 copy-done.3
  15.8 1.1 bitcast_bitcast_fusion
  16.9 195.6 %all-reduce.14.cloned.1.call-done = f32[4,2,5120]{2,1,0:T(2,128)} async-done(((f32[4,2,5120]{2,1,0:T(2,128)}), f32[4,2,5120]{2,1,0:T(2,128)}) %all-reduce.14.cloned.1.call-update) | async-done | bytes 163856 | tf_op jit(solution)/shard_map/psum | solution.py:125
  212.4 1.1 multiply_reduce_fusion.1
  213.5 1.1 multiply_convert_fusion.1
  214.6 1.0 fusion.77
  215.8 181.4 %all-reduce.16.cloned.1.call-done = f32[8,7168]{1,0:T(8,128)} async-done(((f32[8,7168]{1,0:T(8,128)}), f32[8,7168]{1,0:T(8,128)}) %all-reduce.16.cloned.1.call-update) | async-done | bytes 229392 | tf_op jit(solution)/shard_map/psum | solution.py:130
  397.2 1.0 add_convert_fusion
  400.1 1.5 fusion.9
  402.4 38.6 %all-gather.9.cloned.1.call-done = f32[8,326,128]{2,1,0:T(8,128)} async-done(((f32[1,326,128]{2,1,0:T(8,128)}), f32[8,326,128]{2,1,0:T(8,128)}) %all-gather.9.cloned.1.call-update) | async-done | bytes 1335312 | tf_op jit(solution)/shard_map/all_gather | solution.py:25
  441.0 0.8 fusion.88
  442.1 2.0 fusion.39
  444.1 0.7 maximum_bitcast_fusion.1
  445.1 0.8 fusion.93
  446.0 38.5 %all-gather.11.cloned.1.call-done = f32[8,326,128]{2,1,0:T(8,128)} async-done(((f32[1,326,128]{2,1,0:T(8,128)}), f32[8,326,128]{2,1,0:T(8,128)}) %all-gather.11.cloned.1.call-update) | async-done | bytes 1335312 | tf_op jit(solution)/shard_map/all_gather | solution.py:25
  484.5 0.8 fusion.87
  485.6 2.0 fusion.18
  487.6 2.1 all-gather.5
  492.8 1.0 convolution_add_fusion.1
  493.9 56.9 %all_gather.27 = f32[4,2,5120]{0,1,2:T(2,128)} all-gather(f32[4,2,40]{0,1,2:T(2,128)S(1)} %copy.230), channel_id=1, replica_groups=mesh['parts'=2,'seq_0'=8,'seq_1'=8,'seq_2'=2] {'seq_0','seq_1','seq_2'}, dimensions={2}, use_global_device_ids=true | all-gather | bytes 165120 | tf_op jit(solution)/shard_map/all_gather | solution.py:191
  550.8 5.6 copy.233
  556.5 7.0 multiply_reduce_fusion
  564.2 1.9 fusion.8
  566.7 1.1 copy.236
  569.3 30.1 %all-reduce.18.cloned.1.call-done = f32[128,4,2,40]{3,1,2,0:T(4,128)} async-done(((f32[128,4,2,40]{3,1,2,0:T(4,128)}), f32[128,4,2,40]{3,1,2,0:T(4,128)}) %all-reduce.18.cloned.1.call-update) | async-done | bytes 163856
  599.4 1.7 constant_dynamic-slice_fusion.2
  603.0 75.6 %all-reduce.20.cloned.1.call-done = f32[64,4,2,40]{3,1,2,0:T(4,128)} async-done(((f32[64,4,2,40]{3,1,2,0:T(4,128)}), f32[64,4,2,40]{3,1,2,0:T(4,128)}) %all-reduce.20.cloned.1.call-update) | async-done | bytes 81936
  678.7 0.8 constant_dynamic-slice_fusion.1
  679.4 29.7 %all-reduce.8 = f32[8,4,2,40]{3,1,2,0:T(4,128)S(1)} all-reduce(f32[8,4,2,40]{3,1,2,0:T(4,128)S(1)} %constant_dynamic-slice_fusion.1), channel_id=7, replica_groups=mesh['parts'=2,'seq_0'=8,'seq_1'=8,'seq_2'=2] {'seq_0'}, use_global_device_ids=true, to_apply=%region_10.11.clone | all-reduce | flops 2560 | bytes 20480
  (137 shorter events, 12.8 us)
Async XLA Ops:
  7.2 557.1 %copy-start = (bf16[128,5120]{1,0:T(8,128)(2,1)S(1)}, bf16[128,5120]{1,0:T(8,128)(2,1)}, u32[]{:S(2)}) copy-start(bf16[128,5120]{1,0:T(8,128)(2,1)} %param.25) | copy-start | bytes 3932164
  7.2 6.6 copy-start.7
  7.2 6.6 copy-start.9
  7.2 6.8 copy-start.2
  7.2 205.2 %all-reduce.14.cloned.1.call-start = ((), (), s32[]{:S(2)}) async-start(), calls=%async_computation | async-start | bytes 327680 | tf_op jit(solution)/shard_map/psum | solution.py:125
  13.7 383.5 %all-reduce.16.cloned.1.call-start = ((), (), s32[]{:S(2)}) async-start(), calls=%async_computation.1 | async-start | bytes 458752 | tf_op jit(solution)/shard_map/psum | solution.py:130
  14.3 1.2 copy-start.3
  15.8 198.8 %copy-start.4 = (bf16[40,7168]{1,0:T(8,128)(2,1)S(1)}, bf16[40,7168]{1,0:T(8,128)(2,1)}, u32[]{:S(2)}) copy-start(bf16[40,7168]{1,0:T(8,128)(2,1)} %param.17) | copy-start | bytes 1720324
  16.9 380.3 %copy-start.6 = (f32[7168]{0:T(1024)S(1)}, f32[7168]{0:T(1024)}, u32[]{:S(2)}) copy-start(f32[7168]{0:T(1024)} %param.18) | copy-start | bytes 86020
  215.7 225.3 %all-gather.9.cloned.1.call-start = ((), (), s32[]{:S(2)}) async-start(), calls=%async_computation.2 | async-start | bytes 1511424 | tf_op jit(solution)/shard_map/all_gather | solution.py:25
  402.3 42.6 %copy-start.8 = (bf16[5120]{0:T(1024)(128)(2,1)S(1)}, bf16[5120]{0:T(1024)(128)(2,1)}, u32[]{:S(2)}) copy-start(bf16[5120]{0:T(1024)(128)(2,1)} %param.22) | copy-start | bytes 30724
  402.3 82.2 %all-gather.11.cloned.1.call-start = ((), (), s32[]{:S(2)}) async-start(), calls=%async_computation.3 | async-start | bytes 1511424 | tf_op jit(solution)/shard_map/all_gather | solution.py:25
  444.8 154.6 %all-reduce.18.cloned.1.call-start = ((), (), s32[]{:S(2)}) async-start(), calls=%async_computation.4 | async-start | bytes 1048576
  491.8 1.0 copy-start.10
  492.8 58.0 %copy-start.5 = (bf16[4,2,5120]{2,1,0:T(2,128)(2,1)}, bf16[4,2,5120]{2,1,0:T(2,128)(2,1)S(1)}, u32[]{:S(2)}) copy-start(bf16[4,2,5120]{2,1,0:T(2,128)(2,1)S(1)} %convert_element_type.84) | copy-start | bytes 245764
  556.5 7.5 %copy-start.1 = (bf16[5120,128]{1,0:T(8,128)(2,1)S(1)}, bf16[5120,128]{1,0:T(8,128)(2,1)}, u32[]{:S(2)}) copy-start(bf16[5120,128]{1,0:T(8,128)(2,1)} %param.23) | copy-start | bytes 3932164
  566.5 1.5 copy-start.13
  566.7 34.4 %copy-start.12 = (u32[256]{0:T(256)S(1)}, u32[256]{0:T(256)}, u32[]{:S(2)}) copy-start(u32[256]{0:T(256)} %constant.90) | copy-start | bytes 3076
  566.7 35.0 %copy-start.11 = (u32[256]{0:T(256)S(1)}, u32[256]{0:T(256)}, u32[]{:S(2)}) copy-start(u32[256]{0:T(256)} %constant.94) | copy-start | bytes 3076
  567.9 110.7 %all-reduce.20.cloned.1.call-start = ((), (), s32[]{:S(2)}) async-start(), calls=%async_computation.5 | async-start | bytes 524288
Sparse Core Ops, SparseCore 0:
  13.8 198.6 all-reduce.13
  215.8 181.3 all-reduce.15
  402.5 38.5 all-gather.8
  444.9 39.5 all-gather.10
  568.1 31.3 all-reduce.17
  601.6 77.0 all-reduce.19
where the time goes:
time: 718 us; the launch traced here: 717 us
  waiting for transfers between devices  560 us (78%)
  blocking collectives  88.7 us (12%)
  local copies, waits for them, and re-layouts  25.4 us (4%)
  other arithmetic  19.2 us (3%)
  between operations  16 us (2%)
  matrix products  7.37 us (1%)
    psum x1, waiting for transfers between devices, body(): stream = lax.psum(partial_rows, SEQ)  196 us
    psum x1, waiting for transfers between devices, body(): joint_summed = lax.psum(joint_partial, SEQ)  181 us
    unnamed x8, waiting for transfers between devices  106 us
    all_gather x2, waiting for transfers between devices, gathered_once(): both, at, found = (lax.all_gather(jnp.concatenate(lines), axis), 0, {})  77.1 us
    all_gather x1, blocking collectives, body(): mid_rows = lax.all_gather(mid_shard, SEQ, axis=2, tiled=True)  56.9 us
    unnamed x1, blocking collectives  29.7 us
  transfers between devices with their start and end apart: 6, of which 6 were waited for; matrix products, arithmetic and copies ran while one was open for 1% of the time, Pallas kernels for 0%

commit v1 on v0

--- a/solution.py
+++ b/solution.py
@@ -127,7 +127,7 @@
     feature_rows = w_qkv.shape[0]
     normed_local = lax.dynamic_slice_in_dim(normed, rank * feature_rows, feature_rows, 1)
     joint_partial = jnp.dot(normed_local, w_qkv, preferred_element_type=jnp.float32)
-    joint_summed = lax.psum(joint_partial, SEQ)
+    joint_summed = lax.psum(lax.psum(joint_partial, ("seq_1", "seq_2")), "seq_0")
     joint = (joint_summed + qkv_bias).astype(jnp.bfloat16).reshape(step_count, batch_count, -1)
     query_part = joint[..., :query_width].reshape(step_count, batch_count, HEADS, HEAD_DIM)
     key_part = joint[..., query_width : query_width + key_width].reshape(

time: 718 us -> 722 us (level)
    psum x1 -> x2, waiting for transfers between devices: 181 us -> 185 us  [the longest x1 106 us: body(): lax.psum(joint_partial, ('seq_1', 'seq_2'))]
    unnamed x8 -> x9, waiting for transfers between devices: 106 us -> 106 us
  transfers between devices with their start and end apart: 6 -> 7, of which waited for: 6 -> 7; matrix products, arithmetic and copies ran while one was open for 1% -> 1% of each run, Pallas kernels for 0% -> 0%
where the time goes in v1:
time: 722 us; the launch traced here: 721 us
  waiting for transfers between devices  564 us (78%)
  blocking collectives  88.7 us (12%)
  local copies, waits for them, and re-layouts  25.4 us (4%)
  other arithmetic  19.2 us (3%)
  between operations  16 us (2%)
  matrix products  7.37 us (1%)
    psum x1, waiting for transfers between devices, body(): stream = lax.psum(partial_rows, SEQ)  196 us
    unnamed x9, waiting for transfers between devices  106 us
    psum x1, waiting for transfers between devices, body(): lax.psum(joint_partial, ('seq_1', 'seq_2'))  106 us
    psum x1, waiting for transfers between devices, body(): lax.psum(lax.psum(joint_partial, ('seq_1', 'seq_2')), 'seq_0')  78.9 us
    all_gather x2, waiting for transfers between devices, gathered_once(): both, at, found = (lax.all_gather(jnp.concatenate(lines), axis), 0, {})  77.3 us
    all_gather x1, blocking collectives, body(): mid_rows = lax.all_gather(mid_shard, SEQ, axis=2, tiled=True)  56.9 us
    unnamed x1, blocking collectives  29.7 us
  transfers between devices with their start and end apart: 7, of which 7 were waited for; matrix products, arithmetic and copies ran while one was open for 1% of the time, Pallas kernels for 0%

profile of v1, /device:TPU:528, one launch (start us, length us, event | category | flops | bytes accessed | tf_op | source)
XLA Modules:
  0.0 721.1 jit_solution(14655656197767530887)
XLA Ops:
  7.3 0.8 compare_and_fusion
  8.3 4.2 gather_fusion
  12.8 0.8 convert_select_fusion
  14.2 1.1 copy-done.3
  15.6 1.1 bitcast_bitcast_fusion
  16.7 195.8 %all-reduce.15.cloned.1.call-done = f32[4,2,5120]{2,1,0:T(2,128)} async-done(((f32[4,2,5120]{2,1,0:T(2,128)}), f32[4,2,5120]{2,1,0:T(2,128)}) %all-reduce.15.cloned.1.call-update) | async-done | bytes 163856 | tf_op jit(solution)/shard_map/psum | solution.py:125
  212.5 1.1 multiply_reduce_fusion.1
  213.6 1.1 multiply_convert_fusion.1
  214.7 1.0 fusion.77
  215.9 105.8 %all-reduce.17.cloned.1.call-done = f32[8,7168]{1,0:T(8,128)} async-done(((f32[8,7168]{1,0:T(8,128)}), f32[8,7168]{1,0:T(8,128)}) %all-reduce.17.cloned.1.call-update) | async-done | bytes 229392 | tf_op jit(solution)/shard_map/psum | solution.py:130
  321.9 78.9 %all-reduce.19.cloned.1.call-done = f32[8,7168]{1,0:T(8,128)} async-done(((f32[8,7168]{1,0:T(8,128)}), f32[8,7168]{1,0:T(8,128)}) %all-reduce.19.cloned.1.call-update) | async-done | bytes 229392 | tf_op jit(solution)/shard_map/psum | solution.py:130
  400.8 1.0 add_convert_fusion
  403.7 1.5 fusion.9
  406.0 38.8 %all-gather.9.cloned.1.call-done = f32[8,326,128]{2,1,0:T(8,128)} async-done(((f32[1,326,128]{2,1,0:T(8,128)}), f32[8,326,128]{2,1,0:T(8,128)}) %all-gather.9.cloned.1.call-update) | async-done | bytes 1335312 | tf_op jit(solution)/shard_map/all_gather | solution.py:25
  444.8 0.8 fusion.88
  445.9 2.0 fusion.39
  448.9 0.8 fusion.93
  449.8 38.5 %all-gather.11.cloned.1.call-done = f32[8,326,128]{2,1,0:T(8,128)} async-done(((f32[1,326,128]{2,1,0:T(8,128)}), f32[8,326,128]{2,1,0:T(8,128)}) %all-gather.11.cloned.1.call-update) | async-done | bytes 1335312 | tf_op jit(solution)/shard_map/all_gather | solution.py:25
  488.3 0.8 fusion.87
  489.4 2.0 fusion.18
  491.4 2.1 all-gather.5
  496.6 1.0 convolution_add_fusion.1
  497.7 56.9 %all_gather.27 = f32[4,2,5120]{0,1,2:T(2,128)} all-gather(f32[4,2,40]{0,1,2:T(2,128)S(1)} %copy.230), channel_id=1, replica_groups=mesh['parts'=2,'seq_0'=8,'seq_1'=8,'seq_2'=2] {'seq_0','seq_1','seq_2'}, dimensions={2}, use_global_device_ids=true | all-gather | bytes 165120 | tf_op jit(solution)/shard_map/all_gather | solution.py:191
  554.6 5.6 copy.233
  560.3 7.0 multiply_reduce_fusion
  568.0 1.9 fusion.8
  570.5 1.1 copy.236
  573.1 30.1 %all-reduce.21.cloned.1.call-done = f32[128,4,2,40]{3,1,2,0:T(4,128)} async-done(((f32[128,4,2,40]{3,1,2,0:T(4,128)}), f32[128,4,2,40]{3,1,2,0:T(4,128)}) %all-reduce.21.cloned.1.call-update) | async-done | bytes 163856
  603.2 1.7 constant_dynamic-slice_fusion.2
  606.8 75.7 %all-reduce.23.cloned.1.call-done = f32[64,4,2,40]{3,1,2,0:T(4,128)} async-done(((f32[64,4,2,40]{3,1,2,0:T(4,128)}), f32[64,4,2,40]{3,1,2,0:T(4,128)}) %all-reduce.23.cloned.1.call-update) | async-done | bytes 81936
  682.6 0.8 constant_dynamic-slice_fusion.1
  683.3 29.7 %all-reduce.8 = f32[8,4,2,40]{3,1,2,0:T(4,128)S(1)} all-reduce(f32[8,4,2,40]{3,1,2,0:T(4,128)S(1)} %constant_dynamic-slice_fusion.1), channel_id=7, replica_groups=mesh['parts'=2,'seq_0'=8,'seq_1'=8,'seq_2'=2] {'seq_0'}, use_global_device_ids=true, to_apply=%region_11.12.clone | all-reduce | flops 2560 | bytes 20480
  (140 shorter events, 13.6 us)
Async XLA Ops:
  7.2 560.9 %copy-start = (bf16[128,5120]{1,0:T(8,128)(2,1)S(1)}, bf16[128,5120]{1,0:T(8,128)(2,1)}, u32[]{:S(2)}) copy-start(bf16[128,5120]{1,0:T(8,128)(2,1)} %param.25) | copy-start | bytes 3932164
  7.2 6.5 copy-start.7
  7.2 6.6 copy-start.9
  7.2 6.6 copy-start.2
  7.2 205.2 %all-reduce.15.cloned.1.call-start = ((), (), s32[]{:S(2)}) async-start(), calls=%async_computation | async-start | bytes 327680 | tf_op jit(solution)/shard_map/psum | solution.py:125
  13.7 308.0 %all-reduce.17.cloned.1.call-start = ((), (), s32[]{:S(2)}) async-start(), calls=%async_computation.1 | async-start | bytes 458752 | tf_op jit(solution)/shard_map/psum | solution.py:130
  14.1 1.2 copy-start.3
  15.6 199.0 %copy-start.4 = (bf16[40,7168]{1,0:T(8,128)(2,1)S(1)}, bf16[40,7168]{1,0:T(8,128)(2,1)}, u32[]{:S(2)}) copy-start(bf16[40,7168]{1,0:T(8,128)(2,1)} %param.17) | copy-start | bytes 1720324
  16.7 384.1 %copy-start.6 = (f32[7168]{0:T(1024)S(1)}, f32[7168]{0:T(1024)}, u32[]{:S(2)}) copy-start(f32[7168]{0:T(1024)} %param.18) | copy-start | bytes 86020
  215.7 185.1 %all-reduce.19.cloned.1.call-start = ((), (), s32[]{:S(2)}) async-start(), calls=%async_computation.2 | async-start | bytes 458752 | tf_op jit(solution)/shard_map/psum | solution.py:130
  321.7 123.1 %all-gather.9.cloned.1.call-start = ((), (), s32[]{:S(2)}) async-start(), calls=%async_computation.3 | async-start | bytes 1511424 | tf_op jit(solution)/shard_map/all_gather | solution.py:25
  405.9 42.8 %copy-start.8 = (bf16[5120]{0:T(1024)(128)(2,1)S(1)}, bf16[5120]{0:T(1024)(128)(2,1)}, u32[]{:S(2)}) copy-start(bf16[5120]{0:T(1024)(128)(2,1)} %param.22) | copy-start | bytes 30724
  405.9 82.4 %all-gather.11.cloned.1.call-start = ((), (), s32[]{:S(2)}) async-start(), calls=%async_computation.4 | async-start | bytes 1511424 | tf_op jit(solution)/shard_map/all_gather | solution.py:25
  448.6 154.6 %all-reduce.21.cloned.1.call-start = ((), (), s32[]{:S(2)}) async-start(), calls=%async_computation.5 | async-start | bytes 1048576
  495.6 1.0 copy-start.10
  496.6 58.0 %copy-start.5 = (bf16[4,2,5120]{2,1,0:T(2,128)(2,1)}, bf16[4,2,5120]{2,1,0:T(2,128)(2,1)S(1)}, u32[]{:S(2)}) copy-start(bf16[4,2,5120]{2,1,0:T(2,128)(2,1)S(1)} %convert_element_type.84) | copy-start | bytes 245764
  560.3 7.5 %copy-start.1 = (bf16[5120,128]{1,0:T(8,128)(2,1)S(1)}, bf16[5120,128]{1,0:T(8,128)(2,1)}, u32[]{:S(2)}) copy-start(bf16[5120,128]{1,0:T(8,128)(2,1)} %param.23) | copy-start | bytes 3932164
  570.3 1.5 copy-start.13
  570.5 34.4 %copy-start.12 = (u32[256]{0:T(256)S(1)}, u32[256]{0:T(256)}, u32[]{:S(2)}) copy-start(u32[256]{0:T(256)} %constant.90) | copy-start | bytes 3076
  570.5 35.0 %copy-start.11 = (u32[256]{0:T(256)S(1)}, u32[256]{0:T(256)}, u32[]{:S(2)}) copy-start(u32[256]{0:T(256)} %constant.94) | copy-start | bytes 3076
  571.7 110.8 %all-reduce.23.cloned.1.call-start = ((), (), s32[]{:S(2)}) async-start(), calls=%async_computation.6 | async-start | bytes 524288
Sparse Core Ops, SparseCore 0:
  13.8 198.6 all-reduce.14
  215.8 105.8 all-reduce.16
  324.1 76.6 all-reduce.18
  406.0 38.7 all-gather.8
  448.7 39.5 all-gather.10
  571.9 31.3 all-reduce.20
  605.5 76.9 all-reduce.22
